TPU v7x, 128 devices: a whole 4x4x4 slice. The times are simulated.
128 devices in a mesh: arow: 8 (over z, core), acol: 16 (over x, y).
Axes of the slice: x: 4, y: 4, z: 4, core: 2. Of those that a mesh axis runs over, the one named last changes fastest.
Arguments:
- row_data: bfloat16 [262144, 128], P(('arow', 'acol')), may hold values from -96 to 96
- row_baseline: int32 [262144], P(('arow', 'acol')), may hold values from 0 to 524287, as said below
- pair_table: int32 [524288, 2], P(('arow', 'acol')), may hold values from 0 to 2047, as said below
- lengths: int32 [524288], P(('arow', 'acol')), may hold values from 1 to 8
- model_vis: bfloat16 [2048, 2048, 128], P('arow', 'acol'), may hold values from -6 to 6
- gains: float32 [2048, 128], P(('arow', 'acol')), may hold values from -6 to 6
Outputs:
- new_gains: float32 [2048, 128], P(('arow', 'acol'))
Inputs may be any that keep to these rules, and one draw needn't show every extreme that they name: `pair_table`: slot j belongs to tile o = j // 4096; its first antenna lies in 256 * (o // 16) to 256 * (o // 16 + 1) - 1, its second in 128 * (o % 16) to 128 * (o % 16 + 1) - 1, and the two differ. `row_baseline`: the rows of one device name slots of one tile at most 64 times; one tile is named exactly 64 times by the rows of every device.
All inputs are finite; a program needn't handle non-finite values.
Results may differ from a plain program's by a relative error of at most 0.0003.
Values may be sent and summed in bfloat16 or wider, within the bound.
A program may use at most 64 MiB of HBM per device.

v0:
```python
import math

import jax
import jax.numpy as jnp
from jax import lax
from jax.sharding import PartitionSpec as P

RIDGE = 1.0


def split_up(array, dim, length):
    before, after = (array.shape[:dim], array.shape[dim + 1 :])
    return jnp.moveaxis(array.reshape(*before, length, -1, *after), dim, 0)


def joined_along(parts, dim):
    parts = jnp.moveaxis(parts, 0, dim)
    shape = parts.shape
    return parts.reshape(*shape[:dim], shape[dim] * shape[dim + 1], *shape[dim + 2 :])


def one_exchange(array, axis, axes, splits, concats):
    sizes = [lax.axis_size(a) for a in axes]
    parts = split_up(array, splits[0], sizes[0])
    parts = jnp.moveaxis(split_up(parts, splits[1] + 1, sizes[1]), 0, 1)
    inside = parts.shape[2:]
    parts = parts.reshape(-1, *inside)
    parts = lax.all_to_all(parts, axis, split_axis=0, concat_axis=0, tiled=True)
    parts = joined_along(parts.reshape(*sizes, *inside), concats[0] + 1)
    return joined_along(parts, concats[1])


def sum_at_owner(array, axis, dim):
    length = lax.axis_size(axis)
    parts = lax.all_to_all(split_up(array, dim, length), axis, 0, 0, tiled=True)
    return jnp.sum(parts, axis=0)


def sent_together(arrays, axis, dim, along):
    both = jnp.concatenate(arrays, axis=along)
    whole, at, finished = (sum_at_owner(both, axis, dim), 0, [])
    for a in arrays:
        finished.append(lax.slice_in_dim(whole, at, at + a.shape[along], axis=along))
        at += a.shape[along]
    return tuple(finished)


def local(row_data, row_baseline, pair_table, lengths, model_vis, gains):
    row_count = lax.axis_size("arow")
    col_count = lax.axis_size("acol")
    devices = row_count * col_count
    count_rows = row_data.shape[0]
    width = row_data.shape[1]
    half = width // 2
    slots = lengths.shape[0]
    capacity = 4 * count_rows // devices
    row_block = model_vis.shape[0]
    col_block = model_vis.shape[1]
    my_row = lax.axis_index("arow")
    my_col = lax.axis_index("acol")
    owner = row_baseline // slots
    local_id = row_baseline - owner * slots
    hits = (owner[:, None] == jnp.arange(devices, dtype=jnp.int32)[None, :]).astype(jnp.bfloat16)
    step_rows = math.gcd(count_rows, 128)
    block_count = count_rows // step_rows
    blocks = hits.reshape(block_count, step_rows, devices)
    positions = jnp.arange(step_rows, dtype=jnp.int32)
    lower = (positions[:, None] > positions[None, :]).astype(jnp.bfloat16)
    within = jnp.einsum("ij,bjd->bid", lower, blocks, preferred_element_type=jnp.float32)
    per_block = jnp.sum(blocks, axis=1, dtype=jnp.float32)
    before = jnp.cumsum(per_block, axis=0) - per_block
    ranking = jnp.sum((within + before[:, None, :]) * blocks.astype(jnp.float32), axis=2).reshape(
        count_rows
    )
    target = owner * capacity + ranking.astype(jnp.int32)
    code = local_id + 1
    codes = jnp.stack([code // 64, code % 64], axis=1).astype(jnp.bfloat16)
    groups = math.gcd(devices, 16)
    span = devices * capacity // groups

    def place(group):
        wanted = group * span + jnp.arange(span, dtype=jnp.int32)
        table = (target[None, :] == wanted[:, None]).astype(jnp.bfloat16)
        placed = jnp.dot(table, row_data, preferred_element_type=jnp.float32).astype(jnp.bfloat16)
        tagged = jnp.dot(table, codes, preferred_element_type=jnp.float32)
        return (placed, tagged)

    outgoing, tags = lax.map(place, jnp.arange(groups, dtype=jnp.int32))
    outgoing = outgoing.reshape(devices * capacity, width)
    labels = (tags[..., 0] * 64.0 + tags[..., 1]).astype(jnp.int32).reshape(devices * capacity) - 1
    arrived, names = (
        one_exchange(
            outgoing.reshape(row_count, col_count, capacity, width),
            ("arow", "acol"),
            ("arow", "acol"),
            (0, 1),
            (0, 1),
        ),
        one_exchange(
            labels.reshape(row_count, col_count, capacity),
            ("arow", "acol"),
            ("arow", "acol"),
            (0, 1),
            (0, 1),
        ),
    )
    arrived = arrived.reshape(devices * capacity, width)
    names = names.reshape(devices * capacity)
    valid = names >= 0
    safe = jnp.clip(names, 0, slots - 1)
    slot_info = jnp.concatenate([pair_table, lengths[:, None]], axis=1)
    found = jnp.take(slot_info, safe, axis=0)
    first = jnp.clip(found[:, 0] - my_row * row_block, 0, row_block - 1)
    second = jnp.clip(found[:, 1] - my_col * col_block, 0, col_block - 1)
    weight = jnp.where(valid, found[:, 2], 0).astype(jnp.float32)
    every = lax.all_gather(gains, ("arow", "acol"), axis=0, tiled=True)
    column_gains = lax.dynamic_slice_in_dim(every, my_col * col_block, col_block, 0)
    pick_col = (second[:, None] == jnp.arange(col_block, dtype=jnp.int32)[None, :]).astype(
        jnp.float32
    )
    row_gain = jnp.dot(
        pick_col, column_gains, precision=lax.Precision.HIGHEST, preferred_element_type=jnp.float32
    )
    model_rows = jnp.take(
        model_vis.reshape(row_block * col_block, width), first * col_block + second, axis=0
    )
    m_re = model_rows[:, :half].astype(jnp.float32)
    m_im = model_rows[:, half:].astype(jnp.float32)
    g_re = row_gain[:, :half]
    g_im = row_gain[:, half:]
    c_re = m_re * g_re + m_im * g_im
    c_im = m_re * g_im - m_im * g_re
    r_re = arrived[:, :half].astype(jnp.float32) * weight[:, None]
    r_im = arrived[:, half:].astype(jnp.float32) * weight[:, None]
    values = jnp.concatenate(
        [
            c_re * r_re - c_im * r_im,
            c_re * r_im + c_im * r_re,
            weight[:, None] * (c_re * c_re + c_im * c_im),
        ],
        axis=1,
    )
    pick_row = (first[None, :] == jnp.arange(row_block, dtype=jnp.int32)[:, None]).astype(
        jnp.float32
    )
    totals = jnp.dot(
        pick_row, values, precision=lax.Precision.HIGHEST, preferred_element_type=jnp.float32
    )
    numer = totals[:, :width]
    denom = totals[:, width:]
    numer, denom = sent_together((numer, denom), "acol", 0, 1)
    return jnp.concatenate(
        [numer[:, :half] / (denom + RIDGE), numer[:, half:] / (denom + RIDGE)], axis=1
    )


def solution(mesh):
    placed = (
        P(("arow", "acol"), None),
        P(("arow", "acol")),
        P(("arow", "acol"), None),
        P(("arow", "acol")),
        P("arow", "acol", None),
        P(("arow", "acol"), None),
    )
    return jax.shard_map(
        local, mesh=mesh, in_specs=placed, out_specs=P(("arow", "acol"), None), check_vma=False
    )
```

profile of v0, /device:TPU:1, one launch (start us, length us, event | category | flops | bytes accessed | tf_op | source)
XLA Modules:
  0.0 243.8 jit_solution(4307944587851729840)
XLA Ops:
  6.5 0.7 all-gather.2.cloned.1.call-update
  7.3 0.7 fusion.50
  8.7 0.7 bitcast_add_fusion
  9.5 70.4 %while.12 = (s32[]{:T(128)}, bf16[16,512,128]{2,1,0:T(8,128)(2,1)}, f32[16,512,2]{1,2,0:T(2,128)S(1)}, s32[2048]{0:T(1024)S(1)}, s32[16]{0:T(128)S(1)}, /*index=...) while((s32[]{:T(128)}, bf16[16,512,128]{2,1,0:T(8,128)(2,1)}, ...), condition=%wide.region_4.5_spmd, body=%wide.region_3.4_spmd.sunk | while | flops 274792960 | bytes 690313 | solution.py:88
  9.5 0.6 dynamic_slice.11
  10.7 0.8 fusion.75
  11.5 2.5 %fusion.74 = bf16[16,512,128]{2,1,0:T(8,128)(2,1)} fusion(bf16[16,512,128]{2,1,0:T(8,128)(2,1)} %get-tuple-element.127, s32[]{:T(128)S(6)} %copy.50, bf16[2048,128]{1,0:T(8,128)(2,1)} %get-tuple-element.140, s32[2048]{0:T(1024)S(1)} %get-tuple-element.138, s32[512]{0:T(512)S(1)} %iota_add_fusion.2), kind=kOutput, calls=%fused_computation.12.clone.1 | convolution fusion | flops 269549568 | bytes 665604 | tf_op jit(solution)/shard_map/while/body/eval_jaxpr/dot_general | solution.py:84
  13.9 0.6 dynamic_slice.11
  15.1 0.8 fusion.75
  15.9 2.5 %fusion.74 = bf16[16,512,128]{2,1,0:T(8,128)(2,1)} fusion(bf16[16,512,128]{2,1,0:T(8,128)(2,1)} %get-tuple-element.127, s32[]{:T(128)S(6)} %copy.50, bf16[2048,128]{1,0:T(8,128)(2,1)} %get-tuple-element.140, s32[2048]{0:T(1024)S(1)} %get-tuple-element.138, s32[512]{0:T(512)S(1)} %iota_add_fusion.2), kind=kOutput, calls=%fused_computation.12.clone.1 | convolution fusion | flops 269549568 | bytes 665604 | tf_op jit(solution)/shard_map/while/body/eval_jaxpr/dot_general | solution.py:84
  19.5 0.8 fusion.75
  20.3 2.5 %fusion.74 = bf16[16,512,128]{2,1,0:T(8,128)(2,1)} fusion(bf16[16,512,128]{2,1,0:T(8,128)(2,1)} %get-tuple-element.127, s32[]{:T(128)S(6)} %copy.50, bf16[2048,128]{1,0:T(8,128)(2,1)} %get-tuple-element.140, s32[2048]{0:T(1024)S(1)} %get-tuple-element.138, s32[512]{0:T(512)S(1)} %iota_add_fusion.2), kind=kOutput, calls=%fused_computation.12.clone.1 | convolution fusion | flops 269549568 | bytes 665604 | tf_op jit(solution)/shard_map/while/body/eval_jaxpr/dot_general | solution.py:84
  22.7 0.6 dynamic_slice.11
  23.9 0.8 fusion.75
  24.7 2.5 %fusion.74 = bf16[16,512,128]{2,1,0:T(8,128)(2,1)} fusion(bf16[16,512,128]{2,1,0:T(8,128)(2,1)} %get-tuple-element.127, s32[]{:T(128)S(6)} %copy.50, bf16[2048,128]{1,0:T(8,128)(2,1)} %get-tuple-element.140, s32[2048]{0:T(1024)S(1)} %get-tuple-element.138, s32[512]{0:T(512)S(1)} %iota_add_fusion.2), kind=kOutput, calls=%fused_computation.12.clone.1 | convolution fusion | flops 269549568 | bytes 665604 | tf_op jit(solution)/shard_map/while/body/eval_jaxpr/dot_general | solution.py:84
  28.3 0.8 fusion.75
  29.1 2.5 %fusion.74 = bf16[16,512,128]{2,1,0:T(8,128)(2,1)} fusion(bf16[16,512,128]{2,1,0:T(8,128)(2,1)} %get-tuple-element.127, s32[]{:T(128)S(6)} %copy.50, bf16[2048,128]{1,0:T(8,128)(2,1)} %get-tuple-element.140, s32[2048]{0:T(1024)S(1)} %get-tuple-element.138, s32[512]{0:T(512)S(1)} %iota_add_fusion.2), kind=kOutput, calls=%fused_computation.12.clone.1 | convolution fusion | flops 269549568 | bytes 665604 | tf_op jit(solution)/shard_map/while/body/eval_jaxpr/dot_general | solution.py:84
  32.7 0.8 fusion.75
  33.5 2.5 %fusion.74 = bf16[16,512,128]{2,1,0:T(8,128)(2,1)} fusion(bf16[16,512,128]{2,1,0:T(8,128)(2,1)} %get-tuple-element.127, s32[]{:T(128)S(6)} %copy.50, bf16[2048,128]{1,0:T(8,128)(2,1)} %get-tuple-element.140, s32[2048]{0:T(1024)S(1)} %get-tuple-element.138, s32[512]{0:T(512)S(1)} %iota_add_fusion.2), kind=kOutput, calls=%fused_computation.12.clone.1 | convolution fusion | flops 269549568 | bytes 665604 | tf_op jit(solution)/shard_map/while/body/eval_jaxpr/dot_general | solution.py:84
  37.1 0.8 fusion.75
  37.9 2.5 %fusion.74 = bf16[16,512,128]{2,1,0:T(8,128)(2,1)} fusion(bf16[16,512,128]{2,1,0:T(8,128)(2,1)} %get-tuple-element.127, s32[]{:T(128)S(6)} %copy.50, bf16[2048,128]{1,0:T(8,128)(2,1)} %get-tuple-element.140, s32[2048]{0:T(1024)S(1)} %get-tuple-element.138, s32[512]{0:T(512)S(1)} %iota_add_fusion.2), kind=kOutput, calls=%fused_computation.12.clone.1 | convolution fusion | flops 269549568 | bytes 665604 | tf_op jit(solution)/shard_map/while/body/eval_jaxpr/dot_general | solution.py:84
  41.5 0.8 fusion.75
  42.3 2.5 %fusion.74 = bf16[16,512,128]{2,1,0:T(8,128)(2,1)} fusion(bf16[16,512,128]{2,1,0:T(8,128)(2,1)} %get-tuple-element.127, s32[]{:T(128)S(6)} %copy.50, bf16[2048,128]{1,0:T(8,128)(2,1)} %get-tuple-element.140, s32[2048]{0:T(1024)S(1)} %get-tuple-element.138, s32[512]{0:T(512)S(1)} %iota_add_fusion.2), kind=kOutput, calls=%fused_computation.12.clone.1 | convolution fusion | flops 269549568 | bytes 665604 | tf_op jit(solution)/shard_map/while/body/eval_jaxpr/dot_general | solution.py:84
  45.9 0.8 fusion.75
  46.7 2.5 %fusion.74 = bf16[16,512,128]{2,1,0:T(8,128)(2,1)} fusion(bf16[16,512,128]{2,1,0:T(8,128)(2,1)} %get-tuple-element.127, s32[]{:T(128)S(6)} %copy.50, bf16[2048,128]{1,0:T(8,128)(2,1)} %get-tuple-element.140, s32[2048]{0:T(1024)S(1)} %get-tuple-element.138, s32[512]{0:T(512)S(1)} %iota_add_fusion.2), kind=kOutput, calls=%fused_computation.12.clone.1 | convolution fusion | flops 269549568 | bytes 665604 | tf_op jit(solution)/shard_map/while/body/eval_jaxpr/dot_general | solution.py:84
  50.3 0.8 fusion.75
  51.1 2.5 %fusion.74 = bf16[16,512,128]{2,1,0:T(8,128)(2,1)} fusion(bf16[16,512,128]{2,1,0:T(8,128)(2,1)} %get-tuple-element.127, s32[]{:T(128)S(6)} %copy.50, bf16[2048,128]{1,0:T(8,128)(2,1)} %get-tuple-element.140, s32[2048]{0:T(1024)S(1)} %get-tuple-element.138, s32[512]{0:T(512)S(1)} %iota_add_fusion.2), kind=kOutput, calls=%fused_computation.12.clone.1 | convolution fusion | flops 269549568 | bytes 665604 | tf_op jit(solution)/shard_map/while/body/eval_jaxpr/dot_general | solution.py:84
  54.7 0.8 fusion.75
  55.5 2.5 %fusion.74 = bf16[16,512,128]{2,1,0:T(8,128)(2,1)} fusion(bf16[16,512,128]{2,1,0:T(8,128)(2,1)} %get-tuple-element.127, s32[]{:T(128)S(6)} %copy.50, bf16[2048,128]{1,0:T(8,128)(2,1)} %get-tuple-element.140, s32[2048]{0:T(1024)S(1)} %get-tuple-element.138, s32[512]{0:T(512)S(1)} %iota_add_fusion.2), kind=kOutput, calls=%fused_computation.12.clone.1 | convolution fusion | flops 269549568 | bytes 665604 | tf_op jit(solution)/shard_map/while/body/eval_jaxpr/dot_general | solution.py:84
  59.1 0.8 fusion.75
  59.9 2.5 %fusion.74 = bf16[16,512,128]{2,1,0:T(8,128)(2,1)} fusion(bf16[16,512,128]{2,1,0:T(8,128)(2,1)} %get-tuple-element.127, s32[]{:T(128)S(6)} %copy.50, bf16[2048,128]{1,0:T(8,128)(2,1)} %get-tuple-element.140, s32[2048]{0:T(1024)S(1)} %get-tuple-element.138, s32[512]{0:T(512)S(1)} %iota_add_fusion.2), kind=kOutput, calls=%fused_computation.12.clone.1 | convolution fusion | flops 269549568 | bytes 665604 | tf_op jit(solution)/shard_map/while/body/eval_jaxpr/dot_general | solution.py:84
  63.5 0.8 fusion.75
  64.3 2.4 %fusion.74 = bf16[16,512,128]{2,1,0:T(8,128)(2,1)} fusion(bf16[16,512,128]{2,1,0:T(8,128)(2,1)} %get-tuple-element.127, s32[]{:T(128)S(6)} %copy.50, bf16[2048,128]{1,0:T(8,128)(2,1)} %get-tuple-element.140, s32[2048]{0:T(1024)S(1)} %get-tuple-element.138, s32[512]{0:T(512)S(1)} %iota_add_fusion.2), kind=kOutput, calls=%fused_computation.12.clone.1 | convolution fusion | flops 269549568 | bytes 665604 | tf_op jit(solution)/shard_map/while/body/eval_jaxpr/dot_general | solution.py:84
  67.9 0.8 fusion.75
  68.7 2.5 %fusion.74 = bf16[16,512,128]{2,1,0:T(8,128)(2,1)} fusion(bf16[16,512,128]{2,1,0:T(8,128)(2,1)} %get-tuple-element.127, s32[]{:T(128)S(6)} %copy.50, bf16[2048,128]{1,0:T(8,128)(2,1)} %get-tuple-element.140, s32[2048]{0:T(1024)S(1)} %get-tuple-element.138, s32[512]{0:T(512)S(1)} %iota_add_fusion.2), kind=kOutput, calls=%fused_computation.12.clone.1 | convolution fusion | flops 269549568 | bytes 665604 | tf_op jit(solution)/shard_map/while/body/eval_jaxpr/dot_general | solution.py:84
  72.3 0.8 fusion.75
  73.1 2.5 %fusion.74 = bf16[16,512,128]{2,1,0:T(8,128)(2,1)} fusion(bf16[16,512,128]{2,1,0:T(8,128)(2,1)} %get-tuple-element.127, s32[]{:T(128)S(6)} %copy.50, bf16[2048,128]{1,0:T(8,128)(2,1)} %get-tuple-element.140, s32[2048]{0:T(1024)S(1)} %get-tuple-element.138, s32[512]{0:T(512)S(1)} %iota_add_fusion.2), kind=kOutput, calls=%fused_computation.12.clone.1 | convolution fusion | flops 269549568 | bytes 665604 | tf_op jit(solution)/shard_map/while/body/eval_jaxpr/dot_general | solution.py:84
  76.7 0.8 fusion.75
  77.5 2.5 %fusion.74 = bf16[16,512,128]{2,1,0:T(8,128)(2,1)} fusion(bf16[16,512,128]{2,1,0:T(8,128)(2,1)} %get-tuple-element.127, s32[]{:T(128)S(6)} %copy.50, bf16[2048,128]{1,0:T(8,128)(2,1)} %get-tuple-element.140, s32[2048]{0:T(1024)S(1)} %get-tuple-element.138, s32[512]{0:T(512)S(1)} %iota_add_fusion.2), kind=kOutput, calls=%fused_computation.12.clone.1 | convolution fusion | flops 269549568 | bytes 665604 | tf_op jit(solution)/shard_map/while/body/eval_jaxpr/dot_general | solution.py:84
  80.1 0.7 sub.59
  80.8 11.5 %all-to-all-start = ((s32[128,1,1,64]{3,2,1,0:T(1,128)}), s32[128,1,1,64]{3,2,1,0:T(1,128)S(1)}, u32[]{:S(2)}, u32[]{:S(2)}) async-start(s32[128,1,1,64]{3,2,1,0:T(1,128)} %bitcast.7), calls=%async_computation | async-start | bytes 131072 | tf_op jit(solution)/shard_map/all_to_all | solution.py:28
  92.4 0.6 copy.35
  93.0 8.9 %all-to-all-done = s32[128,1,1,64]{3,2,1,0:T(1,128)S(1)} async-done(((s32[128,1,1,64]{3,2,1,0:T(1,128)}), s32[128,1,1,64]{3,2,1,0:T(1,128)S(1)}, u32[]{:S(2)}, u32[]{:S(2)}) %all-to-all-start) | async-done | bytes 32800 | tf_op jit(solution)/shard_map/all_to_all | solution.py:28
  101.9 5.5 %all-to-all-start.1 = ((bf16[128,1,1,64,128]{4,3,2,1,0:T(8,128)(2,1)}), bf16[128,1,1,64,128]{4,3,2,1,0:T(8,128)(2,1)}, u32[]{:S(2)}, u32[]{:S(2)}) async-start(bf16[128,1,1,64,128]{4,3,2,1,0:T(8,128)(2,1)} %bitcast.77), calls=%async_computation.1 | async-start | bytes 4194304 | tf_op jit(solution)/shard_map/all_to_all | solution.py:28
  107.5 5.5 %min.48 = s32[8192,1]{1,0:T(8,128)} reshape(s32[8,16,1,64]{3,1,0,2:T(8,128)S(1)} %bitcast.79) | data formatting | bytes 65536 | tf_op jit(solution)/shard_map/jit(clip)/min | solution.py:110
  113.0 3.3 %fusion.29 = s32[8192]{0:T(1024)S(1)} fusion(s32[8192,1]{1,0:T(8,128)} %min.48), kind=kLoop, calls=%fused_computation.25 | loop fusion | flops 24576 | bytes 65536 | tf_op jit(solution)/shard_map/jit(_take)/jit(_where)/select_n | solution.py:112
  116.4 27.7 %gather_fusion = s32[8192,3]{1,0:T(8,128)} fusion(s32[4096,3]{1,0:T(8,128)S(1)} %copy.35, s32[8192]{0:T(1024)S(1)} %broadcast_clamp_fusion.2), kind=kCustom, calls=%fused_computation | custom fusion | bytes 229376 | tf_op jit(solution)/shard_map/jit(_take)/gather | solution.py:112
  144.1 6.2 %broadcast_select_fusion = s32[8192,3]{1,0:T(8,128)S(1)} fusion(s32[8192,3]{1,0:T(8,128)} %gather_fusion, pred[8192]{0:T(1024)(128)(4,1)S(1)} %compare_and_fusion), kind=kLoop, calls=%fused_computation.51 | loop fusion | flops 24576 | bytes 204800 | tf_op jit(solution)/shard_map/jit(_take)/select_n | solution.py:112
  150.3 3.2 %and_reduce_fusion = pred[8192]{0:T(1024)(128)(4,1)S(1)} fusion(s32[]{:T(128)S(6)} %mul.110, s32[8192,3]{1,0:T(8,128)S(1)} %broadcast_select_fusion, s32[]{:T(128)S(6)} %mul.107), kind=kLoop, calls=%fused_computation.36 | loop fusion | flops 98304 | bytes 73736 | tf_op jit(solution)/shard_map/jit(_take)/and | solution.py:124
  153.5 4.7 %fusion.36 = (s32[8192]{0:T(1024)S(1)}, s32[8192]{0:T(1024)S(1)}, s32[8192]{0:T(1024)S(1)}) fusion(s32[8192,3]{1,0:T(8,128)S(1)} %broadcast_select_fusion, s32[]{:T(128)S(6)} %mul.107, s32[]{:T(128)S(6)} %mul.110), kind=kLoop, calls=%fused_computation.37 | loop fusion | flops 73728 | bytes 163848 | tf_op jit(solution)/shard_map/jit(clip)/min | solution.py:113
  158.2 4.7 %ge.48 = pred[8192,1]{1,0:T(8,128)(4,1)S(1)} reshape(pred[8,16,1,64]{3,1,0,2:T(8,128)(4,1)S(1)} %bitcast.83) | data formatting | bytes 16384 | tf_op jit(solution)/shard_map/ge | solution.py:109
  162.9 4.4 %fusion.31 = f32[8192]{0:T(1024)S(1)} fusion(pred[8192,1]{1,0:T(8,128)(4,1)S(1)} %ge.48, s32[8192,3]{1,0:T(8,128)} %copy-done), kind=kLoop, calls=%fused_computation.28 | loop fusion | flops 16384 | bytes 73728 | tf_op jit(solution)/shard_map/convert_element_type | solution.py:115
  167.3 26.4 %gather_fusion.1 = bf16[8192,128]{1,0:T(8,128)(2,1)S(1)} fusion(bf16[32768,128]{1,0:T(8,128)(2,1)} %bitcast.76, s32[8192]{0:T(1024)S(1)} %broadcast_clamp_fusion.1), kind=kCustom, calls=%fused_computation.1 | custom fusion | bytes 4227072 | tf_op jit(solution)/shard_map/jit(_take)/gather | solution.py:124
  193.7 3.2 %copy.36 = bf16[8192,128]{0,1:T(8,128)(2,1)} copy(bf16[8192,128]{1,0:T(8,128)(2,1)S(1)} %gather_fusion.1) | data formatting | bytes 4194304 | tf_op jit(solution)/shard_map/jit(_take)/gather | solution.py:124
  196.9 3.2 %broadcast_select_fusion.1 = bf16[8192,128]{0,1:T(8,128)(2,1)} fusion(bf16[8192,128]{0,1:T(8,128)(2,1)} %copy.36, pred[8192]{0:T(1024)(128)(4,1)S(1)} %and_reduce_fusion), kind=kLoop, calls=%fused_computation.52 | loop fusion | flops 1048576 | bytes 4202496 | tf_op jit(solution)/shard_map/jit(_take)/select_n | solution.py:124
  200.2 5.5 %fusion.35 = f32[8192,128]{0,1:T(8,128)} fusion(s32[8192]{0:T(1024)S(1)} %get-tuple-element.47, f32[2048,128]{1,0:T(8,128)} %all-gather.2.cloned.1.call-done, s32[]{:T(128)S(6)} %select_n.61), kind=kOutput, calls=%fused_computation.35 | convolution fusion | flops 1611661312 | bytes 4292612 | tf_op jit(solution)/shard_map/dot_general | solution.py:121
  205.7 4.3 %fusion.61 = (bf16[8192,64]{1,0:T(8,128)(2,1)S(1)}, bf16[8192,64]{1,0:T(8,128)(2,1)}) fusion(bf16[8192,128]{1,0:T(8,128)(2,1)} %bitcast.23), kind=kLoop, calls=%fused_computation.100 | loop fusion | bytes 4194304 | tf_op jit(solution)/shard_map/slice | solution.py:133
  209.9 0.8 copy.43
  210.8 1.9 copy.44
  212.7 3.9 %multiply_subtract_fusion = (f32[8192,64]{0,1:T(8,128)S(1)}, f32[8192,64]{0,1:T(8,128)S(1)}, f32[8192,64]{0,1:T(8,128)S(1)}) fusion(bf16[8192,64]{0,1:T(8,128)(2,1)S(1)} %copy.44, bf16[8192,64]{0,1:T(8,128)(2,1)S(1)} %copy.43, f32[8192]{0:T(1024)S(1)} %fusion.31, f32[8192,128]{0,1:T(8,128)} %fusion.35, bf16[8192,128]{0,1:T(8,128)(2,1)} %broadcast_select_fusion.1), kind=kLoop, calls=%fused_computation.47 | loop fusion | flops 7864320 | bytes 14712832 | tf_op jit(solution)/shard_map/sub | solution.py:137
  216.6 0.8 multiply_add_fusion
  217.3 4.8 %fusion.23 = f32[256,192]{1,0:T(8,128)S(1)} fusion(f32[8192,64]{0,1:T(8,128)S(1)} %get-tuple-element.66, f32[8192,64]{0,1:T(8,128)S(1)} %get-tuple-element.65, f32[8192,64]{0,1:T(8,128)S(1)} %get-tuple-element.62, s32[8192]{0:T(1024)S(1)} %get-tuple-element.45), kind=kOutput, calls=%fused_computation.19 | convolution fusion | flops 4837081088 | bytes 6520832 | tf_op jit(solution)/shard_map/dot_general | solution.py:146
  222.2 14.0 %all_to_all.15 = f32[16,16,192]{2,1,0:T(8,128)S(1)} all-to-all(f32[16,16,192]{2,1,0:T(8,128)S(1)} %bitcast.82), channel_id=1, replica_groups=mesh['arow'=8,'acol'=16] {'acol'}, dimensions={0} | all-to-all | bytes 393216 | tf_op jit(solution)/shard_map/all_to_all | solution.py:35
  236.3 0.7 pad_maximum_fusion.1
  (58 shorter events, 8.4 us)
Async XLA Ops:
  6.5 193.6 %all-gather.2.cloned.1.call-start = ((), (), s32[]{:S(2)}) async-start(), calls=%async_computation.3 | async-start | bytes 1056768 | tf_op jit(solution)/shard_map/all_gather | solution.py:116
  9.5 82.8 %copy-start.1 = (s32[4096,2]{0,1:T(2,128)S(1)}, s32[4096,2]{0,1:T(2,128)}, u32[]{:S(2)}) copy-start(s32[4096,2]{0,1:T(2,128)} %param.10) | copy-start | bytes 98308
  9.5 82.8 %copy-start.2 = (s32[4096]{0:T(1024)S(1)}, s32[4096]{0:T(1024)}, u32[]{:S(2)}) copy-start(s32[4096]{0:T(1024)} %param.11) | copy-start | bytes 49156
  80.8 21.1 %all-to-all-start = ((s32[128,1,1,64]{3,2,1,0:T(1,128)}), s32[128,1,1,64]{3,2,1,0:T(1,128)S(1)}, u32[]{:S(2)}, u32[]{:S(2)}) async-start(s32[128,1,1,64]{3,2,1,0:T(1,128)} %bitcast.7), calls=%async_computation | async-start | bytes 131072 | tf_op jit(solution)/shard_map/all_to_all | solution.py:28
  101.9 103.8 %all-to-all-start.1 = ((bf16[128,1,1,64,128]{4,3,2,1,0:T(8,128)(2,1)}), bf16[128,1,1,64,128]{4,3,2,1,0:T(8,128)(2,1)}, u32[]{:S(2)}, u32[]{:S(2)}) async-start(bf16[128,1,1,64,128]{4,3,2,1,0:T(8,128)(2,1)} %bitcast.77), calls=%async_computation.1 | async-start | bytes 4194304 | tf_op jit(solution)/shard_map/all_to_all | solution.py:28
  150.3 3.2 %copy-start = (s32[8192,3]{1,0:T(8,128)}, s32[8192,3]{1,0:T(8,128)S(1)}, u32[]{:S(2)}) copy-start(s32[8192,3]{1,0:T(8,128)S(1)} %broadcast_select_fusion) | copy-start | bytes 294916
Sparse Core Ops, SparseCore 0:
  10.1 67.1 all-gather.1
where the time goes:
time: 246 us; the launch traced here: 244 us
  local copies, waits for them, and re-layouts  84.8 us (34%)
  matrix products  63 us (26%)
  other arithmetic  32.5 us (13%)
  starting transfers between devices  17 us (7%)
  blocking collectives  14 us (6%)
  between operations  13.7 us (6%)
  waiting for transfers between devices  9.59 us (4%)
  loops' own time  9.34 us (4%)
    dot_general x16, matrix products, place(): jnp.dot(table, row_data, preferred_element_type=jnp.float32)  39.3 us
    gather x2, local copies, waits for them, and re-layouts, local(): jnp.take(model_vis.reshape(row_block * col_block, width), first * col_blo...  29.6 us
    gather x1, local copies, waits for them, and re-layouts, local(): found = jnp.take(slot_info, safe, axis=0)  27.7 us
    all_to_all x2, starting transfers between devices, one_exchange(): parts = lax.all_to_all(parts, axis, split_axis=0, concat_axis=0, tiled=True)  17 us
    all_to_all x1, blocking collectives, sum_at_owner(): parts = lax.all_to_all(split_up(array, dim, length), axis, 0, 0, tiled=True)  14 us
    dot_general x16, matrix products, place(): tagged = jnp.dot(table, codes, preferred_element_type=jnp.float32)  12.9 us
    select_n x2, other arithmetic, local(): found = jnp.take(slot_info, safe, axis=0)  9.55 us
    another operation x1, loops' own time, local(): outgoing, tags = lax.map(place, jnp.arange(groups, dtype=jnp.int32))  9.34 us
  transfers between devices with their start and end apart: 3, of which 1 were waited for; matrix products, arithmetic and copies ran while one was open for 67% of the time, Pallas kernels for 0%

commit v1 on v0

v1 whole, which is shorter than its diff:
```python
import functools

import jax
import jax.numpy as jnp
from jax import lax
from jax.experimental import pallas as pl
from jax.experimental.pallas import tpu as pltpu
from jax.sharding import PartitionSpec as P

MESH = pl.DeviceIdType.MESH
RIDGE = 1.0
F32 = jnp.float32
BF16 = jnp.bfloat16
I32 = jnp.int32

ROWS = 2048
CAP = 64
SLOTS = 4096
AR = 256
AC = 128
HALF = 64
DEVICES = 128
GROUPS = 32
CHUNKS = 8
DY = (2, 1, 3, 0)
SELF_GROUP = 20
SELF_SLOT = 83


def far_first(a):
    return lax.rem(2 + 3 * a, 4)


def place():
    row = lax.axis_index("arow")
    col = lax.axis_index("acol")
    return row, col


def destination(g):
    row, col = place()
    z = lax.rem(row // 2 + far_first(g // 8), 4)
    core = lax.rem(row + lax.rem(g, 2), 2)
    x = lax.rem(col // 4 + far_first(lax.rem(g // 2, 4)), 4)
    return 2 * z + core, x


def iota(shape, dim):
    return lax.broadcasted_iota(I32, shape, dim)


def one_hot(match):
    return jnp.where(match, F32(1), F32(0)).astype(BF16)


def split_two(value):
    high = value.astype(BF16)
    return high, (value - high.astype(F32)).astype(BF16)


def kernel(
    x_hbm, rb_hbm, pair_hbm, len_hbm, m_hbm, g_hbm, out_ref,
    x_v, rb_v, pair_v, len_v, mb_v, mf_v, idx_v, idx_s, msel, xt, tgt,
    send, sendc, recv, recvc, gcol, cre, cim, den, codes, lhs, cb, acc,
    part, got,
    in_sem, m_sem, idx_sem, g_sem, gs_sem, d_ssem, d_rsem, c_ssem, c_rsem, r_ssem, r_rsem,
):
    row, col = place()
    me = row * 16 + col
    y = lax.rem(col, 4)

    barrier = pltpu.get_barrier_semaphore()

    @pl.loop(0, GROUPS)
    def _(g):
        r2, x2 = destination(g)
        for dy in DY:
            y2 = lax.rem(y + dy, 4)
            if dy:
                pl.semaphore_signal(barrier, 1, device_id=(r2, 4 * x2 + y2), device_id_type=MESH)
            else:
                @pl.when(g != SELF_GROUP)
                def _():
                    pl.semaphore_signal(barrier, 1, device_id=(r2, 4 * x2 + y2), device_id_type=MESH)

    loads = [
        pltpu.make_async_copy(rb_hbm, rb_v, in_sem.at[0]),
        pltpu.make_async_copy(pair_hbm, pair_v, in_sem.at[1]),
        pltpu.make_async_copy(x_hbm, x_v, in_sem.at[2]),
        pltpu.make_async_copy(len_hbm, len_v, in_sem.at[3]),
    ]
    for load in loads:
        load.start()
    m_loads = [
        pltpu.make_async_copy(m_hbm.at[pl.ds(j * 4096, 4096)], mb_v.at[pl.ds(j * 4096, 4096)], m_sem.at[j])
        for j in range(8)
    ]
    for load in m_loads:
        load.start()

    loads[0].wait()
    slots = rb_v[...]
    owner = slots // SLOTS
    local = slots - owner * SLOTS + 1
    owner_t = owner.astype(F32).T
    lower = one_hot(iota((256, 256), 0) > iota((256, 256), 1))
    ones = jnp.ones((128, 128), BF16)
    lane = iota((128, 128), 1).astype(F32)
    before = jnp.zeros((1, 128), F32)
    for b in range(8):
        own = jnp.concatenate(
            [jnp.broadcast_to(owner_t[:, 2 * b + h : 2 * b + h + 1], (128, 128)) for h in range(2)], axis=0
        )
        hit = jnp.where(own == jnp.concatenate([lane, lane], axis=0), F32(1), F32(0))
        within = jnp.dot(lower, hit.astype(BF16), preferred_element_type=F32)
        rank = jnp.dot((hit * (within + before)).astype(BF16), ones, preferred_element_type=F32)
        tgt[b * 256 : b * 256 + 256, :] = (own * CAP + rank).astype(I32)
        before = before + within[255:256, :] + hit[255:256, :]

    loads[1].wait()
    for k in range(32):
        p = pair_v[0:1, k * 128 : k * 128 + 128] - row * AR
        q = pair_v[1:2, k * 128 : k * 128 + 128] - col * AC
        idx_v[k : k + 1, :] = jnp.clip(p * AC + q, 0, AR * AC - 1)
    idx_copy = pltpu.make_async_copy(idx_v, idx_s, idx_sem)
    idx_copy.start()

    loads[2].wait()
    sub = iota((16, 128), 0)
    for b in range(16):
        xt[0:128, b * 128 : b * 128 + 128] = x_v[b * 128 : b * 128 + 128, :].T
        code = local[b : b + 1, :]
        high = code // 64
        digits = jnp.where(sub == 0, high, jnp.where(sub == 1, code - high * 64, 0))
        xt[128:144, b * 128 : b * 128 + 128] = digits.astype(F32).astype(BF16)

    pl.semaphore_wait(barrier, DEVICES - 1)

    g_col = me // 8
    g_at = pl.ds(pl.multiple_of(lax.rem(me, 8) * 16, 16), 16)
    for r2 in range(8):
        @pl.when(jnp.logical_or(row != r2, col != g_col))
        def _():
            pltpu.make_async_remote_copy(
                src_ref=g_hbm, dst_ref=gcol.at[g_at], send_sem=gs_sem, recv_sem=g_sem,
                device_id=(r2, g_col), device_id_type=MESH,
            ).start()

    @pl.when(col == g_col)
    def _():
        pltpu.make_async_copy(g_hbm, gcol.at[g_at], g_sem).start()

    low_lanes = iota((HALF, 128), 1) < HALF

    def pack(g):
        r2, x2 = destination(g)
        group = r2 * 4 + x2
        total = None
        for kb in range(8):
            rows = tgt[kb * 256 : kb * 256 + 256, :]
            hot = jnp.concatenate(
                [one_hot(rows == iota((256, 128), 1) + (group * 256 + h * 128)) for h in range(2)], axis=1
            )
            term = jnp.dot(xt[:, kb * 256 : kb * 256 + 256], hot, preferred_element_type=F32)
            total = term if total is None else total + term
        for h in range(2):
            re = total[0:64, h * 128 : h * 128 + 128]
            im = total[64:128, h * 128 : h * 128 + 128]
            send[group * 4 + 2 * h] = jnp.where(low_lanes, re, pltpu.roll(im, 64, 1)).astype(BF16)
            send[group * 4 + 2 * h + 1] = jnp.where(low_lanes, pltpu.roll(re, 64, 1), im).astype(BF16)
            code = total[128:129, h * 128 : h * 128 + 128] * 64.0 + total[129:130, h * 128 : h * 128 + 128]
            sendc[group * 2 + h] = code.astype(I32) - 1

    def ship(g):
        r2, x2 = destination(g)
        group = r2 * 4 + x2
        chunk = g // 4
        for k, dy in enumerate(DY):
            y2 = lax.rem(y + dy, 4)

            def go():
                pltpu.make_async_remote_copy(
                    src_ref=sendc.at[group * 2 + y2 // 2], dst_ref=recvc.at[g * 4 + k],
                    send_sem=c_ssem, recv_sem=c_rsem.at[chunk],
                    device_id=(r2, 4 * x2 + y2), device_id_type=MESH,
                ).start()
                pltpu.make_async_remote_copy(
                    src_ref=send.at[group * 4 + y2], dst_ref=recv.at[g * 4 + k],
                    send_sem=d_ssem, recv_sem=d_rsem.at[chunk],
                    device_id=(r2, 4 * x2 + y2), device_id_type=MESH,
                ).start()

            if dy:
                go()
            else:
                pl.when(g != SELF_GROUP)(go)

    pack(jnp.int32(0))

    @pl.loop(1, GROUPS)
    def _(g):
        pack(g)
        ship(g - 1)

    ship(jnp.int32(GROUPS - 1))
    recv[SELF_SLOT] = send[me]
    recvc[SELF_SLOT] = sendc[me // 2]

    for j in range(8):
        m_loads[j].wait()

        @pl.loop(0, 16)
        def _(b):
            at = pl.ds(pl.multiple_of(j * 4096 + b * 256, 256), 256)
            mf_v[at, :] = mb_v[at, :].astype(F32)

    idx_copy.wait()

    @pl.loop(0, 64)
    def _(b):
        for u in range(64):
            i = idx_s[b // 2, lax.rem(b, 2) * 64 + u]
            msel[pl.ds(b * 64 + u, 1), :] = mf_v[pl.ds(i, 1), :]

    loads[3].wait()
    pltpu.make_async_copy(gcol, gcol, g_sem).wait()
    gains_two = jnp.concatenate(split_two(gcol[...].T), axis=0)
    for k in range(32):
        at = slice(k * 128, k * 128 + 128)
        q = pair_v[1:2, at] - col * AC
        picked = jnp.dot(gains_two, one_hot(iota((128, 128), 0) == q), preferred_element_type=F32)
        g_re = picked[0:64] + picked[128:192]
        g_im = picked[64:128] + picked[192:256]
        model = msel[at, :].T
        m_re = model[0:64]
        m_im = model[64:128]
        c_re = m_re * g_re + m_im * g_im
        c_im = m_re * g_im - m_im * g_re
        w = len_v[k : k + 1, :].astype(F32)
        cre[:, at] = w * c_re
        cim[:, at] = w * c_im
        den[:, at] = w * (c_re * c_re + c_im * c_im)

    acc[...] = jnp.zeros_like(acc)
    lhs[128:144, :] = jnp.ones((16, 1024), BF16)
    odd = lax.rem(col, 2) == 1
    first_lanes = iota((1, 128), 1) < HALF

    def add_chunk(j, senders):
        pltpu.make_async_copy(recv.at[pl.ds(0, senders)], recv.at[pl.ds(0, senders)], d_rsem.at[j]).wait()
        pltpu.make_async_copy(recvc.at[pl.ds(0, senders)], recvc.at[pl.ds(0, senders)], c_rsem.at[j]).wait()
        for s in range(8):
            a = recv[j * 16 + 2 * s].astype(F32)
            b = recv[j * 16 + 2 * s + 1].astype(F32)
            at = slice(s * 128, s * 128 + 128)
            lhs[0:64, at] = jnp.where(low_lanes, a, pltpu.roll(b, 64, 1)).astype(BF16)
            lhs[64:128, at] = jnp.where(low_lanes, pltpu.roll(a, 64, 1), b).astype(BF16)
            ca = recvc[j * 16 + 2 * s]
            cbb = recvc[j * 16 + 2 * s + 1]
            even_codes = jnp.where(first_lanes, ca, pltpu.roll(cbb, 64, 1))
            odd_codes = jnp.where(first_lanes, pltpu.roll(ca, 64, 1), cbb)
            codes[s : s + 1, :] = jnp.where(odd, odd_codes, even_codes)
        codes_t = codes[...].astype(F32).T
        for s in range(8):
            cb[s * 128 : s * 128 + 128, :] = jnp.broadcast_to(codes_t[:, s : s + 1], (128, 128)).astype(I32)
        for nb in range(16):
            total = None
            for kb in range(4):
                rows = cb[kb * 256 : kb * 256 + 256, :]
                hot = jnp.concatenate(
                    [one_hot(rows == iota((256, 128), 1) + (nb * 256 + h * 128)) for h in range(2)], axis=1
                )
                term = jnp.dot(lhs[:, kb * 256 : kb * 256 + 256], hot, preferred_element_type=F32)
                total = term if total is None else total + term
            acc[:, nb * 256 : nb * 256 + 256] += total

    @pl.loop(0, CHUNKS)
    def _(j):
        @pl.when(j == SELF_SLOT // 16)
        def _():
            add_chunk(j, 15)

        @pl.when(j != SELF_SLOT // 16)
        def _():
            add_chunk(j, 16)

    total = None
    for nb in range(16):
        at = slice(nb * 256, nb * 256 + 256)
        d_re = acc[0:64, at]
        d_im = acc[64:128, at]
        v = jnp.concatenate(
            [cre[:, at] * d_re - cim[:, at] * d_im, cre[:, at] * d_im + cim[:, at] * d_re, den[:, at] * acc[128:129, at]],
            axis=0,
        )
        both = jnp.concatenate(split_two(v), axis=0)
        p = pair_v[0:1, at] - row * AR
        hot = one_hot(iota((AR, 256), 0) == p)
        term = lax.dot_general(hot, both, (((1,), (1,)), ((), ())), preferred_element_type=F32)
        total = term if total is None else total + term
    numer = total[:, 0:128] + total[:, 192:320]
    denom = total[:, 128:192] + total[:, 320:384]
    wide = jnp.concatenate([denom, denom], axis=1)
    eight = iota((8, 128), 1) < HALF
    for b in range(16):
        part[b, 0:16, :] = numer[b * 16 : b * 16 + 16]
        part[b, 16:24, :] = jnp.where(eight, wide[b * 16 : b * 16 + 8], wide[b * 16 + 8 : b * 16 + 16])

    for k in range(1, 16):
        x2 = lax.rem(col // 4 + k // 4, 4)
        y2 = lax.rem(y + k, 4)
        pltpu.make_async_remote_copy(
            src_ref=part.at[4 * x2 + y2], dst_ref=got.at[k], send_sem=r_ssem, recv_sem=r_rsem,
            device_id=(row, 4 * x2 + y2), device_id_type=MESH,
        ).start()
    result = part[col]
    pltpu.make_async_copy(got.at[pl.ds(1, 15)], got.at[pl.ds(1, 15)], r_rsem).wait()
    for k in range(1, 16):
        result = result + got[k]
    d8 = result[16:24] + RIDGE
    d8r = pltpu.roll(d8, 64, 1)
    out_ref[0:8, :] = result[0:8] / jnp.where(eight, d8, d8r)
    out_ref[8:16, :] = result[8:16] / jnp.where(eight, d8r, d8)

    pltpu.make_async_copy(send.at[pl.ds(0, 127)], send.at[pl.ds(0, 127)], d_ssem).wait()
    pltpu.make_async_copy(recvc.at[pl.ds(0, 127)], recvc.at[pl.ds(0, 127)], c_ssem).wait()
    pltpu.make_async_copy(part.at[pl.ds(0, 15)], part.at[pl.ds(0, 15)], r_ssem).wait()

    @pl.when(col == g_col)
    def _():
        pltpu.make_async_copy(gcol.at[pl.ds(0, 112)], gcol.at[pl.ds(0, 112)], gs_sem).wait()

    @pl.when(col != g_col)
    def _():
        pltpu.make_async_copy(gcol, gcol, gs_sem).wait()


def local_step(row_data, row_baseline, pair_table, lengths, model_vis, gains):
    any_space = pl.BlockSpec(memory_space=pl.ANY)
    vm = pltpu.VMEM
    dma = pltpu.SemaphoreType.DMA
    return pl.pallas_call(
        kernel,
        out_shape=jax.ShapeDtypeStruct((16, 128), F32),
        in_specs=[any_space] * 6,
        out_specs=pl.BlockSpec(memory_space=pltpu.VMEM),
        scratch_shapes=[
            vm((ROWS, 128), BF16), vm((16, 128), I32), vm((2, SLOTS), I32), vm((32, 128), I32),
            vm((AR * AC, 128), BF16), vm((AR * AC, 128), F32),
            vm((32, 128), I32), pltpu.SMEM((32, 128), I32), vm((SLOTS, 128), F32),
            vm((144, ROWS), BF16), vm((ROWS, 128), I32),
            vm((DEVICES, HALF, 128), BF16), vm((DEVICES // 2, 1, 128), I32),
            vm((DEVICES, HALF, 128), BF16), vm((DEVICES, 1, 128), I32),
            vm((AC, 128), F32),
            vm((HALF, SLOTS), F32), vm((HALF, SLOTS), F32), vm((HALF, SLOTS), F32),
            vm((8, 128), I32), vm((144, 1024), BF16), vm((1024, 128), I32), vm((144, SLOTS), F32),
            vm((16, 24, 128), F32), vm((16, 24, 128), F32),
            dma((4,)), dma((8,)), dma, dma, dma, dma, dma((CHUNKS,)), dma, dma((CHUNKS,)), dma, dma,
        ],
        compiler_params=pltpu.CompilerParams(
            collective_id=0, has_side_effects=True, vmem_limit_bytes=60 * 2**20
        ),
    )(
        row_data,
        row_baseline.reshape(16, 128),
        pair_table.T,
        lengths.reshape(32, 128),
        model_vis.reshape(AR * AC, 128),
        gains,
    )


def solution(mesh):
    rows = P(("arow", "acol"))
    placed = (
        P(("arow", "acol"), None),
        rows,
        P(("arow", "acol"), None),
        rows,
        P("arow", "acol", None),
        P(("arow", "acol"), None),
    )
    return jax.shard_map(
        local_step, mesh=mesh, in_specs=placed, out_specs=P(("arow", "acol"), None), check_vma=False
    )
```

time: 246 us -> 68.4 us (0.28)
  local copies, waits for them, and re-layouts: 84.8 us -> 1.3 us
  Pallas kernels: 0 us -> 66.9 us
  matrix products: 63 us -> 0 us
  other arithmetic: 32.5 us -> 0 us
  starting transfers between devices: 17 us -> 0 us
  blocking collectives: 14 us -> 0 us
  between operations: 13.7 us -> 0.01 us
  waiting for transfers between devices: 9.59 us -> 0 us
  loops' own time: 9.34 us -> 0 us
    pallas_call x0 -> x1, Pallas kernels: none -> 66.9 us  [local_step(): pl.pallas_call(kernel, out_shape=jax.ShapeDtypeStruct((16, 128), F32), in...]
    dot_general x35 -> x0, matrix products: 63 us -> none  [the longest x16 39.3 us: place(): jnp.dot(table, row_data, preferred_element_type=jnp.float32)]
    gather x3 -> x0, local copies, waits for them, and re-layouts: 57.3 us -> none  [the longest x2 29.6 us: local(): jnp.take(model_vis.reshape(row_block * col_block, width), first * col_blo...]
    all_to_all x2 -> x0, starting transfers between devices: 17 us -> none  [one_exchange(): parts = lax.all_to_all(parts, axis, split_axis=0, concat_axis=0, tiled=True)]
    all_to_all x1 -> x0, blocking collectives: 14 us -> none  [sum_at_owner(): parts = lax.all_to_all(split_up(array, dim, length), axis, 0, 0, tiled=True)]
    select_n x3 -> x0, other arithmetic: 12.8 us -> none  [the longest x2 9.55 us: local(): found = jnp.take(slot_info, safe, axis=0)]
    another operation x1 -> x0, loops' own time: 9.34 us -> none  [local(): outgoing, tags = lax.map(place, jnp.arange(groups, dtype=jnp.int32))]
    all_to_all x2 -> x0, waiting for transfers between devices: 8.88 us -> none  [one_exchange(): parts = lax.all_to_all(parts, axis, split_axis=0, concat_axis=0, tiled=True)]
  transfers between devices with their start and end apart: 3 -> 0, of which waited for: 1 -> 0; matrix products, arithmetic and copies ran while one was open for 67% -> 0% of each run, Pallas kernels for 0% -> 0%
where the time goes in v1:
time: 68.4 us; the launch traced here: 68.3 us
  Pallas kernels  66.9 us (98%)
  local copies, waits for them, and re-layouts  1.3 us (2%)
    pallas_call x1, Pallas kernels, local_step(): pl.pallas_call(kernel, out_shape=jax.ShapeDtypeStruct((16, 128), F32), in...  66.9 us

profile of v1, /device:TPU:1, one launch (start us, length us, event | category | flops | bytes accessed | tf_op | source)
XLA Modules:
  0.0 68.3 jit_solution(7324948037071028457)
XLA Ops:
  0.0 66.9 %shard_map.64 = f32[16,128]{1,0:T(8,128)} custom-call(bf16[2048,128]{1,0:T(8,128)(2,1)} %x_hbm.1, s32[16,128]{1,0:T(8,128)} %bitcast.7, s32[2,4096]{1,0:T(2,128)} %bitcast.5, s32[32,128]{1,0:T(8,128)} %bitcast.6, bf16[32768,128]{1,0:T(8,128)(2,1)} %bitcast.4, f32[16,128]{1,0:T(8,128)} %g_hbm.1), custom_call_target="tpu_custom_call" | custom-call | tf_op jit(solution)/shard_map/pallas_call | solution.py:342
  67.0 1.3 %copy.8 = f32[16,128]{1,0:T(8,128)} copy(f32[16,128]{1,0:T(8,128)} %shard_map.64) | data formatting | bytes 16384

commit v2 on v1

v2 whole, which is shorter than its diff:
```python
import itertools

import jax
import jax.numpy as jnp
from jax import lax
from jax.experimental import pallas as pl
from jax.experimental.pallas import tpu as pltpu
from jax.sharding import PartitionSpec as P

MESH = pl.DeviceIdType.MESH
RIDGE = 1.0
F32 = jnp.float32
BF16 = jnp.bfloat16
I32 = jnp.int32

ROWS = 2048
CAP = 64
SLOTS = 4096
AR = 256
AC = 128
HALF = 64
DEVICES = 128
CHUNKS = 8
SELF = 127


def place():
    row = lax.axis_index("arow")
    col = lax.axis_index("acol")
    return row, col


def near_first():
    hops = (0, 1, 2, 1)

    def loads(offset):
        load = [0] * 6
        for axis, d in enumerate((offset[0], offset[2], offset[3])):
            if d != 3:
                load[2 * axis] += min(d, 1)
            if d > 1:
                load[2 * axis + 1] += 1
        return load

    left = [o for o in itertools.product(range(4), range(2), range(4), range(4)) if any(o)]
    order, total = [], [0] * 6
    while left:
        near = min(hops[o[0]] + hops[o[2]] + hops[o[3]] for o in left)

        def cost(o):
            after = [t + n for t, n in zip(total, loads(o))]
            return max(after), sum(a * a for a in after), o

        best = min((o for o in left if hops[o[0]] + hops[o[2]] + hops[o[3]] == near), key=cost)
        left.remove(best)
        order.append(best)
        total = [t + n for t, n in zip(total, loads(best))]
    return order + [(0, 0, 0, 0)]


ORDER = near_first()


def offset_of(owner):
    row, col = place()
    z = (owner // 32 - row // 2) & 3
    core = (owner // 16 - row) & 1
    x = (owner // 4 - col // 4) & 3
    return 32 * z + 16 * core + 4 * x + ((owner - col) & 3)


def each_tile(places, act):
    row, col = place()
    rows = [[2 * lax.rem(row // 2 + z, 4) + lax.rem(row + core, 2) for core in range(2)] for z in range(4)]
    xs = [4 * lax.rem(col // 4 + d, 4) for d in range(4)]
    ys = [lax.rem(col + d, 4) for d in range(4)]
    for pos in places:
        if pos != SELF:
            z, core, x, y = ORDER[pos]
            act(pos, (rows[z][core], xs[x] + ys[y]))


def iota(shape, dim):
    return lax.broadcasted_iota(I32, shape, dim)


def one_hot(match):
    return jnp.where(match, F32(1), F32(0)).astype(BF16)


def split_two(value):
    high = value.astype(BF16)
    return high, (value - high.astype(F32)).astype(BF16)


def kernel(
    x_hbm, rb_hbm, pair_hbm, len_hbm, m_hbm, g_hbm, order_hbm, out_ref,
    order_v, x_v, rb_v, pair_v, len_v, mb_v, mf_v, idx_v, idx_s, msel, xt, tgt,
    send, sendc, recv, recvc, gcol, cre, cim, den, codes, lhs, cb, acc,
    part, got, raw, gains_two,
    in_sem, m_sem, idx_sem, g_sem, gs_sem, g2_sem, gs2_sem, d_ssem, d_rsem, c_ssem, c_rsem, r_ssem, r_rsem,
):
    row, col = place()
    me = row * 16 + col

    loads = [
        pltpu.make_async_copy(rb_hbm, rb_v, in_sem.at[0]),
        pltpu.make_async_copy(pair_hbm, pair_v, in_sem.at[1]),
        pltpu.make_async_copy(x_hbm, x_v, in_sem.at[2]),
        pltpu.make_async_copy(len_hbm, len_v, in_sem.at[3]),
        pltpu.make_async_copy(order_hbm, order_v, in_sem.at[4]),
    ]
    for load in loads:
        load.start()
    m_loads = [
        pltpu.make_async_copy(m_hbm.at[pl.ds(j * 4096, 4096)], mb_v.at[pl.ds(j * 4096, 4096)], m_sem.at[j])
        for j in range(8)
    ]
    for load in m_loads:
        load.start()

    barrier = pltpu.get_barrier_semaphore()

    each_tile(
        range(DEVICES - 1, -1, -1),
        lambda pos, peer: pl.semaphore_signal(barrier, 1, device_id=peer, device_id_type=MESH),
    )

    loads[0].wait()
    slots = rb_v[...]
    owner = slots // SLOTS
    local = slots - owner * SLOTS + 1
    owner_t = offset_of(owner).astype(F32).T
    loads[4].wait()
    places = order_v[...]
    lower = one_hot(iota((256, 256), 0) > iota((256, 256), 1))
    spread = jnp.where(iota((256, 128), 0) < 128, F32(1), F32(CAP)).astype(BF16)
    lane = iota((256, 128), 1).astype(F32)
    before = jnp.zeros((1, 128), F32)
    for b in range(8):
        own = jnp.concatenate(
            [jnp.broadcast_to(owner_t[:, 2 * b + h : 2 * b + h + 1], (128, 128)) for h in range(2)], axis=0
        )
        hit = jnp.where(own == places, F32(1), F32(0))
        within = jnp.dot(lower, hit.astype(BF16), preferred_element_type=F32)
        two = jnp.concatenate([(hit * (within + before)).astype(BF16), (hit * lane).astype(BF16)], axis=1)
        tgt[b * 256 : b * 256 + 256, :] = jnp.dot(two, spread, preferred_element_type=F32).astype(I32)
        before = before + within[255:256, :] + hit[255:256, :]

    loads[1].wait()
    for k in range(32):
        p = pair_v[0:1, k * 128 : k * 128 + 128] - row * AR
        q = pair_v[1:2, k * 128 : k * 128 + 128] - col * AC
        idx_v[k : k + 1, :] = jnp.clip(p * AC + q, 0, AR * AC - 1)
    idx_copy = pltpu.make_async_copy(idx_v, idx_s, idx_sem)
    idx_copy.start()

    loads[2].wait()
    sub = iota((16, 128), 0)
    for b in range(16):
        xt[0:128, b * 128 : b * 128 + 128] = x_v[b * 128 : b * 128 + 128, :].T
        code = local[b : b + 1, :]
        high = code // 64
        digits = jnp.where(sub == 0, high, jnp.where(sub == 1, code - high * 64, 0))
        xt[128:144, b * 128 : b * 128 + 128] = digits.astype(F32).astype(BF16)

    acc[...] = jnp.zeros_like(acc)
    lhs[128:144, :] = jnp.ones((16, 1024), BF16)
    low_lanes = iota((HALF, 128), 1) < HALF

    def multiply(c, k):
        total = None
        for kb in range(8):
            rows = tgt[kb * 256 : kb * 256 + 256, :]
            hot = jnp.concatenate(
                [one_hot(rows == iota((256, 128), 1) + (c * 1024 + k * 256 + h * 128)) for h in range(2)], axis=1
            )
            term = jnp.dot(xt[:, kb * 256 : kb * 256 + 256], hot, preferred_element_type=F32)
            total = term if total is None else total + term
        raw[k] = total

    def arrange(c, k):
        for h in range(2):
            at = slice(h * 128, h * 128 + 128)
            re = raw[k, 0:64, at]
            im = pltpu.roll(raw[k, 64:128, at], 64, 1)
            send[c * 16 + k * 4 + 2 * h] = jnp.where(low_lanes, re, im).astype(BF16)
            send[c * 16 + k * 4 + 2 * h + 1] = jnp.where(low_lanes, im, re).astype(BF16)
            code = raw[k, 128:129, at] * 64.0 + raw[k, 129:130, at]
            sendc[c * 8 + k * 2 + h] = code.astype(I32) - 1

    def pack(c, beside):
        for k in range(4):
            multiply(c, k)
            beside(k)
            if k:
                arrange(c, k - 1)
        arrange(c, 3)

    def ship(c):
        def go(pos, peer):
            pltpu.make_async_remote_copy(
                src_ref=sendc.at[pos // 2], dst_ref=recvc.at[pos],
                send_sem=c_ssem, recv_sem=c_rsem.at[c], device_id=peer, device_id_type=MESH,
            ).start()
            pltpu.make_async_remote_copy(
                src_ref=send.at[pos], dst_ref=recv.at[pos],
                send_sem=d_ssem, recv_sem=d_rsem.at[c], device_id=peer, device_id_type=MESH,
            ).start()

        each_tile(range(c * 16, c * 16 + 16), go)

    def widen(at, count):
        at = pl.ds(pl.multiple_of(at, 1024), count)
        mf_v[at, :] = mb_v[at, :].astype(F32)

    def wait_model(j):
        at = pl.ds(pl.multiple_of(j * 4096, 4096), 4096)
        pltpu.make_async_copy(m_hbm.at[at], mb_v.at[at], m_sem.at[j]).wait()

    pack(0, lambda k: None)
    pl.semaphore_wait(barrier, DEVICES - 1)

    g_row = lax.rem(me, 8)
    g_col = me // 8
    g_at = pl.ds(pl.multiple_of(g_row * 16, 16), 16)
    g_mine = jnp.logical_and(row == g_row, col == g_col)

    @pl.when(g_mine)
    def _():
        pltpu.make_async_copy(g_hbm, gcol.at[g_at], g_sem).start()

    @pl.when(jnp.logical_not(g_mine))
    def _():
        pltpu.make_async_remote_copy(
            src_ref=g_hbm, dst_ref=gcol.at[g_at], send_sem=gs_sem, recv_sem=g_sem,
            device_id=(g_row, g_col), device_id_type=MESH,
        ).start()

    ship(0)

    @pl.loop(1, CHUNKS)
    def _(c):
        wait_model(c)
        pack(c, lambda k: widen(c * 4096 + k * 1024, 1024))

        @pl.when(c == 4)
        def _():
            pltpu.make_async_copy(gcol.at[pl.ds(0, 16)], gcol.at[pl.ds(0, 16)], g_sem).wait()
            my_gains = gcol.at[pl.ds(pl.multiple_of(row * 16, 16), 16)]
            for k in range(1, 8):
                pltpu.make_async_remote_copy(
                    src_ref=my_gains, dst_ref=my_gains, send_sem=gs2_sem, recv_sem=g2_sem,
                    device_id=(lax.rem(row + k, 8), col), device_id_type=MESH,
                ).start()

        for k in range(1, CHUNKS):
            @pl.when(c == k)
            def _():
                ship(k)

    wait_model(0)
    widen(0, 4096)
    idx_copy.wait()
    loads[3].wait()

    first_lanes = iota((1, 128), 1) < HALF

    def gather(block, u0, count):
        for u in range(u0, u0 + count):
            i = idx_s[block, u]
            msel[pl.ds(block * 128 + u, 1), :] = mf_v[pl.ds(i, 1), :]

    def slot_terms(block, gains_two):
        at = pl.ds(pl.multiple_of(block * 128, 128), 128)
        q = pair_v[1:2, at] - col * AC
        picked = jnp.dot(gains_two, one_hot(iota((128, 128), 0) == q), preferred_element_type=F32)
        g_re = picked[0:64] + picked[128:192]
        g_im = picked[64:128] + picked[192:256]
        model = msel[at, :].T
        m_re = model[0:64]
        m_im = model[64:128]
        c_re = m_re * g_re + m_im * g_im
        c_im = m_re * g_im - m_im * g_re
        w = len_v[pl.ds(block, 1), :].astype(F32)
        cre[:, at] = w * c_re
        cim[:, at] = w * c_im
        den[:, at] = w * (c_re * c_re + c_im * c_im)

    def arrived(j, senders):
        pltpu.make_async_copy(recv.at[pl.ds(0, senders)], recv.at[pl.ds(0, senders)], d_rsem.at[j]).wait()
        pltpu.make_async_copy(recvc.at[pl.ds(0, senders)], recvc.at[pl.ds(0, senders)], c_rsem.at[j]).wait()

    def add_chunk(j, beside):
        for s in range(8):
            a = recv[j * 16 + 2 * s].astype(F32)
            b = recv[j * 16 + 2 * s + 1].astype(F32)
            at = slice(s * 128, s * 128 + 128)
            lhs[0:64, at] = jnp.where(low_lanes, a, b).astype(BF16)
            lhs[64:128, at] = pltpu.roll(jnp.where(low_lanes, b, a), 64, 1).astype(BF16)
            codes[s : s + 1, :] = jnp.where(first_lanes, recvc[j * 16 + 2 * s], recvc[j * 16 + 2 * s + 1])
        codes_t = codes[...].astype(F32).T
        for s in range(8):
            cb[s * 128 : s * 128 + 128, :] = jnp.broadcast_to(codes_t[:, s : s + 1], (128, 128)).astype(I32)
        for nb in range(16):
            total = None
            for kb in range(4):
                rows = cb[kb * 256 : kb * 256 + 256, :]
                hot = jnp.concatenate(
                    [one_hot(rows == iota((256, 128), 1) + (nb * 256 + h * 128)) for h in range(2)], axis=1
                )
                term = jnp.dot(lhs[:, kb * 256 : kb * 256 + 256], hot, preferred_element_type=F32)
                total = term if total is None else total + term
            acc[:, nb * 256 : nb * 256 + 256] += total
            beside(nb)

    @pl.loop(0, 4)
    def _(j):
        arrived(j, 16)
        add_chunk(j, lambda nb: gather(j * 8 + nb // 2, nb % 2 * 64, 64))

    recv[SELF] = send[SELF]
    recvc[SELF] = sendc[SELF // 2]
    pltpu.make_async_copy(gcol.at[pl.ds(0, 112)], gcol.at[pl.ds(0, 112)], g2_sem).wait()
    gains_two[...] = jnp.concatenate(split_two(gcol[...].T), axis=0)

    @pl.loop(4, 7)
    def _(j):
        arrived(j, 16)

        def beside(nb):
            if nb < 11:
                slot_terms(jnp.minimum((j - 4) * 11 + nb, 31), gains_two[...])

        add_chunk(j, beside)

    arrived(7, 15)
    add_chunk(7, lambda nb: None)

    total = None
    for nb in range(16):
        at = slice(nb * 256, nb * 256 + 256)
        d_re = acc[0:64, at]
        d_im = acc[64:128, at]
        v = jnp.concatenate(
            [cre[:, at] * d_re - cim[:, at] * d_im, cre[:, at] * d_im + cim[:, at] * d_re, den[:, at] * acc[128:129, at]],
            axis=0,
        )
        both = jnp.concatenate(split_two(v), axis=0)
        p = pair_v[0:1, at] - row * AR
        hot = one_hot(iota((AR, 256), 0) == p)
        term = lax.dot_general(hot, both, (((1,), (1,)), ((), ())), preferred_element_type=F32)
        total = term if total is None else total + term
    numer = total[:, 0:128] + total[:, 192:320]
    denom = total[:, 128:192] + total[:, 320:384]
    wide = jnp.concatenate([denom, denom], axis=1)
    eight = iota((8, 128), 1) < HALF
    for b in range(16):
        part[b, 0:16, :] = numer[b * 16 : b * 16 + 16]
        part[b, 16:24, :] = jnp.where(eight, wide[b * 16 : b * 16 + 8], wide[b * 16 + 8 : b * 16 + 16])

    for k in range(1, 16):
        x2 = lax.rem(col // 4 + k // 4, 4)
        y2 = lax.rem(lax.rem(col, 4) + k, 4)
        pltpu.make_async_remote_copy(
            src_ref=part.at[4 * x2 + y2], dst_ref=got.at[k], send_sem=r_ssem, recv_sem=r_rsem,
            device_id=(row, 4 * x2 + y2), device_id_type=MESH,
        ).start()
    result = part[col]
    pltpu.make_async_copy(got.at[pl.ds(1, 15)], got.at[pl.ds(1, 15)], r_rsem).wait()
    for k in range(1, 16):
        result = result + got[k]
    d8 = result[16:24] + RIDGE
    d8r = pltpu.roll(d8, 64, 1)
    out_ref[0:8, :] = result[0:8] / jnp.where(eight, d8, d8r)
    out_ref[8:16, :] = result[8:16] / jnp.where(eight, d8r, d8)

    pltpu.make_async_copy(send.at[pl.ds(0, 127)], send.at[pl.ds(0, 127)], d_ssem).wait()
    pltpu.make_async_copy(recvc.at[pl.ds(0, 127)], recvc.at[pl.ds(0, 127)], c_ssem).wait()
    pltpu.make_async_copy(part.at[pl.ds(0, 15)], part.at[pl.ds(0, 15)], r_ssem).wait()

    pltpu.make_async_copy(gcol.at[pl.ds(0, 112)], gcol.at[pl.ds(0, 112)], gs2_sem).wait()

    @pl.when(jnp.logical_not(g_mine))
    def _():
        pltpu.make_async_copy(gcol.at[pl.ds(0, 16)], gcol.at[pl.ds(0, 16)], gs_sem).wait()


def local_step(row_data, row_baseline, pair_table, lengths, model_vis, gains):
    any_space = pl.BlockSpec(memory_space=pl.ANY)
    vm = pltpu.VMEM
    dma = pltpu.SemaphoreType.DMA
    return pl.pallas_call(
        kernel,
        out_shape=jax.ShapeDtypeStruct((16, 128), F32),
        in_specs=[any_space] * 7,
        out_specs=pl.BlockSpec(memory_space=pltpu.VMEM),
        scratch_shapes=[
            vm((1, 128), F32), vm((ROWS, 128), BF16), vm((16, 128), I32), vm((2, SLOTS), I32), vm((32, 128), I32),
            vm((AR * AC, 128), BF16), vm((AR * AC, 128), F32),
            vm((32, 128), I32), pltpu.SMEM((32, 128), I32), vm((SLOTS, 128), F32),
            vm((144, ROWS), BF16), vm((ROWS, 128), I32),
            vm((DEVICES, HALF, 128), BF16), vm((DEVICES // 2, 1, 128), I32),
            vm((DEVICES, HALF, 128), BF16), vm((DEVICES, 1, 128), I32),
            vm((AC, 128), F32),
            vm((HALF, SLOTS), F32), vm((HALF, SLOTS), F32), vm((HALF, SLOTS), F32),
            vm((8, 128), I32), vm((144, 1024), BF16), vm((1024, 128), I32), vm((144, SLOTS), F32),
            vm((16, 24, 128), F32), vm((16, 24, 128), F32),
            vm((4, 144, 256), F32), vm((256, 128), BF16),
            dma((5,)), dma((8,)), dma, dma, dma, dma, dma, dma, dma((CHUNKS,)), dma, dma((CHUNKS,)), dma, dma,
        ],
        compiler_params=pltpu.CompilerParams(
            collective_id=0, has_side_effects=True, vmem_limit_bytes=60 * 2**20
        ),
    )(
        row_data,
        row_baseline.reshape(16, 128),
        pair_table.T,
        lengths.reshape(32, 128),
        model_vis.reshape(AR * AC, 128),
        gains,
        jnp.array([[32 * z + 16 * core + 4 * x + y for z, core, x, y in ORDER]], F32),
    )


def solution(mesh):
    rows = P(("arow", "acol"))
    placed = (
        P(("arow", "acol"), None),
        rows,
        P(("arow", "acol"), None),
        rows,
        P("arow", "acol", None),
        P(("arow", "acol"), None),
    )
    return jax.shard_map(
        local_step, mesh=mesh, in_specs=placed, out_specs=P(("arow", "acol"), None), check_vma=False
    )
```

time: 68.4 us -> 56.1 us (0.82)
  Pallas kernels: 66.9 us -> 54.6 us
    pallas_call x1, Pallas kernels: 66.9 us -> 54.6 us  [local_step(): pl.pallas_call(kernel, out_shape=jax.ShapeDtypeStruct((16, 128), F32), in...]
where the time goes in v2:
time: 56.1 us; the launch traced here: 55.9 us
  Pallas kernels  54.6 us (97%)
  local copies, waits for them, and re-layouts  1.3 us (2%)
    pallas_call x1, Pallas kernels, local_step(): pl.pallas_call(kernel, out_shape=jax.ShapeDtypeStruct((16, 128), F32), in...  54.6 us
    unnamed x1, local copies, waits for them, and re-layouts  1.3 us

profile of v2, /device:TPU:1, one launch (start us, length us, event | category | flops | bytes accessed | tf_op | source)
XLA Modules:
  0.0 55.9 jit_solution(13337250246863513534)
XLA Ops:
  0.0 54.6 %shard_map.73 = f32[16,128]{1,0:T(8,128)} custom-call(bf16[2048,128]{1,0:T(8,128)(2,1)} %x_hbm.1, s32[16,128]{1,0:T(8,128)} %bitcast.7, s32[2,4096]{1,0:T(2,128)} %bitcast.5, s32[32,128]{1,0:T(8,128)} %bitcast.6, bf16[32768,128]{1,0:T(8,128)(2,1)} %bitcast.4, f32[16,128]{1,0:T(8,128)} %g_hbm.1, f32[1,128]{1,0:T(1,128)} %constant.2.clone.order_hbm), custom_call_target="tpu_custom_call" | custom-call | tf_op jit(solution)/shard_map/pallas_call | solution.py:393
  54.6 1.3 %copy.9 = f32[16,128]{1,0:T(8,128)} copy(f32[16,128]{1,0:T(8,128)} %shard_map.73) | data formatting | bytes 16384

commit v3 on v2

--- a/solution.py
+++ b/solution.py
@@ -21,6 +21,7 @@
 HALF = 64
 DEVICES = 128
 CHUNKS = 8
+LATE = 120
 SELF = 127
 
 
@@ -95,7 +96,7 @@
 
 def kernel(
     x_hbm, rb_hbm, pair_hbm, len_hbm, m_hbm, g_hbm, order_hbm, out_ref,
-    order_v, x_v, rb_v, pair_v, len_v, mb_v, mf_v, idx_v, idx_s, msel, xt, tgt,
+    order_v, g_v, x_v, rb_v, pair_v, len_v, mb_v, mf_v, idx_v, idx_s, msel, xt, tgt,
     send, sendc, recv, recvc, gcol, cre, cim, den, codes, lhs, cb, acc,
     part, got, raw, gains_two,
     in_sem, m_sem, idx_sem, g_sem, gs_sem, g2_sem, gs2_sem, d_ssem, d_rsem, c_ssem, c_rsem, r_ssem, r_rsem,
@@ -109,6 +110,7 @@
         pltpu.make_async_copy(x_hbm, x_v, in_sem.at[2]),
         pltpu.make_async_copy(len_hbm, len_v, in_sem.at[3]),
         pltpu.make_async_copy(order_hbm, order_v, in_sem.at[4]),
+        pltpu.make_async_copy(g_hbm, g_v, in_sem.at[5]),
     ]
     for load in loads:
         load.start()
@@ -142,9 +144,15 @@
             [jnp.broadcast_to(owner_t[:, 2 * b + h : 2 * b + h + 1], (128, 128)) for h in range(2)], axis=0
         )
         hit = jnp.where(own == places, F32(1), F32(0))
-        within = jnp.dot(lower, hit.astype(BF16), preferred_element_type=F32)
+        rows = slice(b * 256, b * 256 + 256)
+        mf_v[rows, :] = hit
+        msel[rows, :] = jnp.dot(lower, hit.astype(BF16), preferred_element_type=F32)
+    for b in range(8):
+        rows = slice(b * 256, b * 256 + 256)
+        hit = mf_v[rows, :]
+        within = msel[rows, :]
         two = jnp.concatenate([(hit * (within + before)).astype(BF16), (hit * lane).astype(BF16)], axis=1)
-        tgt[b * 256 : b * 256 + 256, :] = jnp.dot(two, spread, preferred_element_type=F32).astype(I32)
+        tgt[rows, :] = jnp.dot(two, spread, preferred_element_type=F32).astype(I32)
         before = before + within[255:256, :] + hit[255:256, :]
 
     loads[1].wait()
@@ -199,13 +207,14 @@
 
     def ship(c):
         def go(pos, peer):
+            part_of = c + (pos >= LATE)
             pltpu.make_async_remote_copy(
                 src_ref=sendc.at[pos // 2], dst_ref=recvc.at[pos],
-                send_sem=c_ssem, recv_sem=c_rsem.at[c], device_id=peer, device_id_type=MESH,
+                send_sem=c_ssem, recv_sem=c_rsem.at[part_of], device_id=peer, device_id_type=MESH,
             ).start()
             pltpu.make_async_remote_copy(
                 src_ref=send.at[pos], dst_ref=recv.at[pos],
-                send_sem=d_ssem, recv_sem=d_rsem.at[c], device_id=peer, device_id_type=MESH,
+                send_sem=d_ssem, recv_sem=d_rsem.at[part_of], device_id=peer, device_id_type=MESH,
             ).start()
 
         each_tile(range(c * 16, c * 16 + 16), go)
@@ -226,14 +235,16 @@
     g_at = pl.ds(pl.multiple_of(g_row * 16, 16), 16)
     g_mine = jnp.logical_and(row == g_row, col == g_col)
 
+    loads[5].wait()
+
     @pl.when(g_mine)
     def _():
-        pltpu.make_async_copy(g_hbm, gcol.at[g_at], g_sem).start()
+        gcol[g_at, :] = g_v[...]
 
     @pl.when(jnp.logical_not(g_mine))
     def _():
         pltpu.make_async_remote_copy(
-            src_ref=g_hbm, dst_ref=gcol.at[g_at], send_sem=gs_sem, recv_sem=g_sem,
+            src_ref=g_v, dst_ref=gcol.at[g_at], send_sem=gs_sem, recv_sem=g_sem,
             device_id=(g_row, g_col), device_id_type=MESH,
         ).start()
 
@@ -246,7 +257,10 @@
 
         @pl.when(c == 4)
         def _():
-            pltpu.make_async_copy(gcol.at[pl.ds(0, 16)], gcol.at[pl.ds(0, 16)], g_sem).wait()
+            @pl.when(jnp.logical_not(g_mine))
+            def _():
+                pltpu.make_async_copy(gcol.at[pl.ds(0, 16)], gcol.at[pl.ds(0, 16)], g_sem).wait()
+
             my_gains = gcol.at[pl.ds(pl.multiple_of(row * 16, 16), 16)]
             for k in range(1, 8):
                 pltpu.make_async_remote_copy(
@@ -259,6 +273,8 @@
             def _():
                 ship(k)
 
+    recv[SELF] = send[SELF]
+    recvc[SELF] = sendc[SELF // 2]
     wait_model(0)
     widen(0, 4096)
     idx_copy.wait()
@@ -291,20 +307,20 @@
         pltpu.make_async_copy(recv.at[pl.ds(0, senders)], recv.at[pl.ds(0, senders)], d_rsem.at[j]).wait()
         pltpu.make_async_copy(recvc.at[pl.ds(0, senders)], recvc.at[pl.ds(0, senders)], c_rsem.at[j]).wait()
 
-    def add_chunk(j, beside):
-        for s in range(8):
-            a = recv[j * 16 + 2 * s].astype(F32)
-            b = recv[j * 16 + 2 * s + 1].astype(F32)
+    def add_chunk(first, pairs, beside):
+        for s in range(pairs):
+            a = recv[first + 2 * s].astype(F32)
+            b = recv[first + 2 * s + 1].astype(F32)
             at = slice(s * 128, s * 128 + 128)
             lhs[0:64, at] = jnp.where(low_lanes, a, b).astype(BF16)
             lhs[64:128, at] = pltpu.roll(jnp.where(low_lanes, b, a), 64, 1).astype(BF16)
-            codes[s : s + 1, :] = jnp.where(first_lanes, recvc[j * 16 + 2 * s], recvc[j * 16 + 2 * s + 1])
+            codes[s : s + 1, :] = jnp.where(first_lanes, recvc[first + 2 * s], recvc[first + 2 * s + 1])
         codes_t = codes[...].astype(F32).T
-        for s in range(8):
+        for s in range(pairs):
             cb[s * 128 : s * 128 + 128, :] = jnp.broadcast_to(codes_t[:, s : s + 1], (128, 128)).astype(I32)
         for nb in range(16):
             total = None
-            for kb in range(4):
+            for kb in range(pairs // 2):
                 rows = cb[kb * 256 : kb * 256 + 256, :]
                 hot = jnp.concatenate(
                     [one_hot(rows == iota((256, 128), 1) + (nb * 256 + h * 128)) for h in range(2)], axis=1
@@ -315,27 +331,30 @@
             beside(nb)
 
     @pl.loop(0, 4)
-    def _(j):
+    def _(t):
+        j = t + t // 3
         arrived(j, 16)
-        add_chunk(j, lambda nb: gather(j * 8 + nb // 2, nb % 2 * 64, 64))
-
-    recv[SELF] = send[SELF]
-    recvc[SELF] = sendc[SELF // 2]
+        add_chunk(j * 16, 8, lambda nb: gather(t * 8 + nb // 2, nb % 2 * 64, 64))
+
+    @pl.loop(0, 2)
+    def _(t):
+        j = 5 - 2 * t
+        arrived(j, 16)
+        add_chunk(j * 16, 8, lambda nb: None)
+
     pltpu.make_async_copy(gcol.at[pl.ds(0, 112)], gcol.at[pl.ds(0, 112)], g2_sem).wait()
     gains_two[...] = jnp.concatenate(split_two(gcol[...].T), axis=0)
 
-    @pl.loop(4, 7)
-    def _(j):
-        arrived(j, 16)
-
-        def beside(nb):
-            if nb < 11:
-                slot_terms(jnp.minimum((j - 4) * 11 + nb, 31), gains_two[...])
-
-        add_chunk(j, beside)
-
-    arrived(7, 15)
-    add_chunk(7, lambda nb: None)
+    def two_blocks(nb):
+        slot_terms(2 * nb, gains_two[...])
+        slot_terms(2 * nb + 1, gains_two[...])
+
+    arrived(6, 16)
+    add_chunk(96, 8, two_blocks)
+    arrived(7, 8)
+    add_chunk(112, 4, lambda nb: None)
+    arrived(8, 7)
+    add_chunk(LATE, 4, lambda nb: None)
 
     total = None
     for nb in range(16):
@@ -396,7 +415,7 @@
         in_specs=[any_space] * 7,
         out_specs=pl.BlockSpec(memory_space=pltpu.VMEM),
         scratch_shapes=[
-            vm((1, 128), F32), vm((ROWS, 128), BF16), vm((16, 128), I32), vm((2, SLOTS), I32), vm((32, 128), I32),
+            vm((1, 128), F32), vm((16, 128), F32), vm((ROWS, 128), BF16), vm((16, 128), I32), vm((2, SLOTS), I32), vm((32, 128), I32),
             vm((AR * AC, 128), BF16), vm((AR * AC, 128), F32),
             vm((32, 128), I32), pltpu.SMEM((32, 128), I32), vm((SLOTS, 128), F32),
             vm((144, ROWS), BF16), vm((ROWS, 128), I32),
@@ -407,7 +426,7 @@
             vm((8, 128), I32), vm((144, 1024), BF16), vm((1024, 128), I32), vm((144, SLOTS), F32),
             vm((16, 24, 128), F32), vm((16, 24, 128), F32),
             vm((4, 144, 256), F32), vm((256, 128), BF16),
-            dma((5,)), dma((8,)), dma, dma, dma, dma, dma, dma, dma((CHUNKS,)), dma, dma((CHUNKS,)), dma, dma,
+            dma((6,)), dma((8,)), dma, dma, dma, dma, dma, dma, dma((CHUNKS + 1,)), dma, dma((CHUNKS + 1,)), dma, dma,
         ],
         compiler_params=pltpu.CompilerParams(
             collective_id=0, has_side_effects=True, vmem_limit_bytes=60 * 2**20

time: 56.1 us -> 52 us (0.927)
  Pallas kernels: 54.6 us -> 50.6 us
    pallas_call x1, Pallas kernels: 54.6 us -> 50.6 us  [local_step(): pl.pallas_call(kernel, out_shape=jax.ShapeDtypeStruct((16, 128), F32), in...]
where the time goes in v3:
time: 52 us; the launch traced here: 51.9 us
  Pallas kernels  50.6 us (97%)
  local copies, waits for them, and re-layouts  1.3 us (2%)
    pallas_call x1, Pallas kernels, local_step(): pl.pallas_call(kernel, out_shape=jax.ShapeDtypeStruct((16, 128), F32), in...  50.6 us
    unnamed x1, local copies, waits for them, and re-layouts  1.3 us

profile of v3, /device:TPU:1, one launch (start us, length us, event | category | flops | bytes accessed | tf_op | source)
XLA Modules:
  0.0 51.9 jit_solution(2689349994258342772)
XLA Ops:
  0.0 50.6 %shard_map.73 = f32[16,128]{1,0:T(8,128)} custom-call(bf16[2048,128]{1,0:T(8,128)(2,1)} %x_hbm.1, s32[16,128]{1,0:T(8,128)} %bitcast.7, s32[2,4096]{1,0:T(2,128)} %bitcast.5, s32[32,128]{1,0:T(8,128)} %bitcast.6, bf16[32768,128]{1,0:T(8,128)(2,1)} %bitcast.4, f32[16,128]{1,0:T(8,128)} %g_hbm.1, f32[1,128]{1,0:T(1,128)} %constant.2.clone.order_hbm), custom_call_target="tpu_custom_call" | custom-call | tf_op jit(solution)/shard_map/pallas_call | solution.py:412
  50.6 1.3 %copy.9 = f32[16,128]{1,0:T(8,128)} copy(f32[16,128]{1,0:T(8,128)} %shard_map.73) | data formatting | bytes 16384

commit v4 on v3

--- a/solution.py
+++ b/solution.py
@@ -342,6 +342,8 @@
         arrived(j, 16)
         add_chunk(j * 16, 8, lambda nb: None)
 
+    arrived(6, 16)
+    add_chunk(96, 8, lambda nb: None)
     pltpu.make_async_copy(gcol.at[pl.ds(0, 112)], gcol.at[pl.ds(0, 112)], g2_sem).wait()
     gains_two[...] = jnp.concatenate(split_two(gcol[...].T), axis=0)
 
@@ -349,10 +351,8 @@
         slot_terms(2 * nb, gains_two[...])
         slot_terms(2 * nb + 1, gains_two[...])
 
-    arrived(6, 16)
-    add_chunk(96, 8, two_blocks)
     arrived(7, 8)
-    add_chunk(112, 4, lambda nb: None)
+    add_chunk(112, 4, two_blocks)
     arrived(8, 7)
     add_chunk(LATE, 4, lambda nb: None)
 
@@ -378,7 +378,8 @@
         part[b, 0:16, :] = numer[b * 16 : b * 16 + 16]
         part[b, 16:24, :] = jnp.where(eight, wide[b * 16 : b * 16 + 8], wide[b * 16 + 8 : b * 16 + 16])
 
-    for k in range(1, 16):
+    hops = (0, 1, 2, 1)
+    for k in sorted(range(1, 16), key=lambda k: -hops[k // 4] - hops[k % 4]):
         x2 = lax.rem(col // 4 + k // 4, 4)
         y2 = lax.rem(lax.rem(col, 4) + k, 4)
         pltpu.make_async_remote_copy(

time: 52 us -> 49.4 us (0.950)
  Pallas kernels: 50.6 us -> 48 us
    pallas_call x1, Pallas kernels: 50.6 us -> 48 us  [local_step(): pl.pallas_call(kernel, out_shape=jax.ShapeDtypeStruct((16, 128), F32), in...]
where the time goes in v4:
time: 49.4 us; the launch traced here: 49.3 us
  Pallas kernels  48 us (97%)
  local copies, waits for them, and re-layouts  1.3 us (3%)
    pallas_call x1, Pallas kernels, local_step(): pl.pallas_call(kernel, out_shape=jax.ShapeDtypeStruct((16, 128), F32), in...  48 us
    unnamed x1, local copies, waits for them, and re-layouts  1.3 us

profile of v4, /device:TPU:1, one launch (start us, length us, event | category | flops | bytes accessed | tf_op | source)
XLA Modules:
  0.0 49.3 jit_solution(14834660382106499337)
XLA Ops:
  0.0 48.0 %shard_map.73 = f32[16,128]{1,0:T(8,128)} custom-call(bf16[2048,128]{1,0:T(8,128)(2,1)} %x_hbm.1, s32[16,128]{1,0:T(8,128)} %bitcast.7, s32[2,4096]{1,0:T(2,128)} %bitcast.5, s32[32,128]{1,0:T(8,128)} %bitcast.6, bf16[32768,128]{1,0:T(8,128)(2,1)} %bitcast.4, f32[16,128]{1,0:T(8,128)} %g_hbm.1, f32[1,128]{1,0:T(1,128)} %constant.2.clone.order_hbm), custom_call_target="tpu_custom_call" | custom-call | tf_op jit(solution)/shard_map/pallas_call | solution.py:413
  48.0 1.3 %copy.9 = f32[16,128]{1,0:T(8,128)} copy(f32[16,128]{1,0:T(8,128)} %shard_map.73) | data formatting | bytes 16384

commit v5 on v4

--- a/solution.py
+++ b/solution.py
@@ -21,7 +21,7 @@
 HALF = 64
 DEVICES = 128
 CHUNKS = 8
-LATE = 120
+LATE = 124
 SELF = 127
 
 
@@ -351,10 +351,10 @@
         slot_terms(2 * nb, gains_two[...])
         slot_terms(2 * nb + 1, gains_two[...])
 
-    arrived(7, 8)
-    add_chunk(112, 4, two_blocks)
-    arrived(8, 7)
-    add_chunk(LATE, 4, lambda nb: None)
+    arrived(7, 12)
+    add_chunk(112, 6, two_blocks)
+    arrived(8, 3)
+    add_chunk(LATE, 2, lambda nb: None)
 
     total = None
     for nb in range(16):

time: 49.4 us -> 49.6 us (level)
  no operation moved by 1% of the time
where the time goes in v5:
time: 49.6 us; the launch traced here: 49.5 us
  Pallas kernels  48.2 us (97%)
  local copies, waits for them, and re-layouts  1.3 us (3%)
    pallas_call x1, Pallas kernels, local_step(): pl.pallas_call(kernel, out_shape=jax.ShapeDtypeStruct((16, 128), F32), in...  48.2 us
    unnamed x1, local copies, waits for them, and re-layouts  1.3 us

profile of v5, /device:TPU:1, one launch (start us, length us, event | category | flops | bytes accessed | tf_op | source)
XLA Modules:
  0.0 49.5 jit_solution(5920683273859636962)
XLA Ops:
  0.0 48.2 %shard_map.73 = f32[16,128]{1,0:T(8,128)} custom-call(bf16[2048,128]{1,0:T(8,128)(2,1)} %x_hbm.1, s32[16,128]{1,0:T(8,128)} %bitcast.7, s32[2,4096]{1,0:T(2,128)} %bitcast.5, s32[32,128]{1,0:T(8,128)} %bitcast.6, bf16[32768,128]{1,0:T(8,128)(2,1)} %bitcast.4, f32[16,128]{1,0:T(8,128)} %g_hbm.1, f32[1,128]{1,0:T(1,128)} %constant.2.clone.order_hbm), custom_call_target="tpu_custom_call" | custom-call | tf_op jit(solution)/shard_map/pallas_call | solution.py:413
  48.2 1.3 %copy.9 = f32[16,128]{1,0:T(8,128)} copy(f32[16,128]{1,0:T(8,128)} %shard_map.73) | data formatting | bytes 16384
